TPU v7x, 32 devices: a whole 2x2x4 slice. The times are simulated.
32 devices in a mesh: dp: 8 (over y, x, core), expert: 4 (over z).
Axes of the slice: x: 2, y: 2, z: 4, core: 2. Of those that a mesh axis runs over, the one named last changes fastest.
Arguments:
- grad_out: bfloat16 [20480, 1024], P(('dp', 'expert')), may hold values from -3 to 3
- hidden_acts: bfloat16 [20480, 384], P(('dp', 'expert')), may hold values from -0.23925781 to 0.23925781
- expert_ids: int32 [20480], P(('dp', 'expert')), may hold values from 0 to 3, as said below
- down_weight: bfloat16 [4, 384, 1024], P('expert'), may hold values from -0.1875 to 0.1875
- error_in: bfloat16 [8, 4, 384, 1024], P('dp', 'expert'), may hold values from -0.8984375 to 0.8984375
- q_prev: float32 [4, 1024, 32], P('expert'), may hold values from -6 to 6
Outputs:
- grad_hidden: bfloat16 [20480, 384], P(('dp', 'expert'))
- left_factor: float32 [4, 384, 32], P('expert')
- right_factor: float32 [4, 1024, 32], P('expert')
- error_out: bfloat16 [8, 4, 384, 1024], P('dp', 'expert')
Inputs may be any that keep to these rules, and one draw needn't show every extreme that they name: `expert_ids`: the rows of one device name each expert at most 320 times; in every replica some expert is named exactly 320 times by the rows of every device of that replica.
All inputs are finite; a program needn't handle non-finite values.
Results may differ from a plain program's by a relative error of at most 0.0004.
Values may be sent and summed in bfloat16 or wider, within the bound.
No kernel may reach another device: no remote copies, remote signals or barrier semaphores. Data moves between devices by JAX's collectives and lax.ppermute only.
A program may use at most 64 MiB of HBM per device.

v0:
```python
import jax
import jax.numpy as jnp
from jax import lax
from jax.sharding import PartitionSpec as P


def place_rows(expert_list, count):
    onehot = (expert_list[:, None] == jnp.arange(count, dtype=jnp.int32)[None, :]).astype(jnp.int32)
    ranks = jnp.cumsum(onehot, axis=0) - 1
    return jnp.sum(ranks * onehot, axis=1)


def orthonormal(block, gram):
    chol = jnp.linalg.cholesky(gram)
    return lax.linalg.triangular_solve(chol, block, left_side=False, lower=True, transpose_a=True)


def shards(grad_out, hidden_acts, expert_ids, down_weight, error_in, q_prev):
    experts = lax.axis_size("expert")
    row_count = grad_out.shape[0]
    capacity = 2 * row_count // experts
    width = grad_out.shape[1]
    hidden_width = hidden_acts.shape[1]
    position = place_rows(expert_ids, experts)
    slot_index = expert_ids * capacity + position
    grad_buffer = jnp.zeros((experts * capacity, width), jnp.bfloat16).at[slot_index].set(grad_out)
    grad_buffer = grad_buffer.reshape(experts, capacity, width)
    hidden_buffer = (
        jnp.zeros((experts * capacity, hidden_width), jnp.bfloat16).at[slot_index].set(hidden_acts)
    )
    hidden_buffer = hidden_buffer.reshape(experts, capacity, hidden_width)
    weight = down_weight[0]
    grad_recv, hidden_recv = (
        lax.all_to_all(grad_buffer, "expert", split_axis=0, concat_axis=0, tiled=True),
        lax.all_to_all(hidden_buffer, "expert", split_axis=0, concat_axis=0, tiled=True),
    )
    product = lax.dot_general(
        grad_recv, weight, (((2,), (1,)), ((), ())), preferred_element_type=jnp.float32
    )
    back = lax.all_to_all(
        product.astype(jnp.bfloat16), "expert", split_axis=0, concat_axis=0, tiled=True
    )
    grads = lax.dot_general(
        hidden_recv.reshape(-1, hidden_width),
        grad_recv.reshape(-1, width),
        (((0,), (0,)), ((), ())),
        preferred_element_type=jnp.float32,
    )
    grad_hidden = back.reshape(experts * capacity, hidden_width)[slot_index]
    merged = grads + error_in[0, 0].astype(jnp.float32)
    highest = lax.Precision.HIGHEST
    left_local = jnp.dot(merged, q_prev[0], precision=highest)
    left_sum = lax.psum(left_local, "dp")
    gram = jnp.dot(left_sum.T, left_sum, precision=highest)
    left_factor = orthonormal(left_sum, gram)
    right_local = lax.dot_general(merged, left_factor, (((0,), (0,)), ((), ())), precision=highest)
    right_factor = lax.psum(right_local, "dp") / lax.axis_size("dp")
    approx = jnp.dot(left_factor, right_factor.T, precision=highest)
    error_out = (merged - approx).astype(jnp.bfloat16)
    return (grad_hidden, left_factor[None], right_factor[None], error_out[None, None])


def solution(mesh):
    placed = (
        P(("dp", "expert"), None),
        P(("dp", "expert"), None),
        P(("dp", "expert")),
        P("expert", None, None),
        P("dp", "expert", None, None),
        P("expert", None, None),
    )
    return jax.shard_map(
        shards,
        mesh=mesh,
        in_specs=placed,
        out_specs=(
            P(("dp", "expert"), None),
            P("expert", None, None),
            P("expert", None, None),
            P("dp", "expert", None, None),
        ),
        check_vma=False,
    )
```

profile of v0, /device:TPU:0, one launch (start us, length us, event | category | flops | bytes accessed | tf_op | source)
XLA Modules:
  0.0 222.1 jit_solution(1954944167356880882)
XLA Ops:
  7.2 0.8 fusion.14
  7.9 1.1 reduce-window.6
  9.5 0.7 fusion.16
  10.3 0.7 compare_select_fusion
  11.0 7.1 %scatter_custom_fusion.1 = bf16[1280,384]{1,0:T(8,128)(2,1)} fusion(s32[640]{0:T(1024)S(1)} %compare_select_fusion, bf16[640,384]{1,0:T(8,128)(2,1)} %param.7, bf16[]{:T(256)} %constant.51.clone.1), kind=kCustom, calls=%fused_computation.10 | custom fusion | bytes 983552 | tf_op jit(solution)/shard_map/scatter | solution.py:29
  18.1 6.3 %all-to-all-start.2 = ((bf16[4,320,384]{2,1,0:T(8,128)(2,1)}), bf16[4,320,384]{2,1,0:T(8,128)(2,1)S(1)}, u32[]{:S(2)}, u32[]{:S(2)}) async-start(bf16[4,320,384]{2,1,0:T(8,128)(2,1)} %bitcast.6), calls=%async_computation.2 | async-start | bytes 1966080 | tf_op jit(solution)/shard_map/all_to_all | solution.py:35
  24.4 8.2 %scatter_custom_fusion = bf16[1280,1024]{1,0:T(8,128)(2,1)} fusion(s32[640]{0:T(1024)S(1)} %compare_select_fusion, bf16[640,1024]{1,0:T(8,128)(2,1)} %param.6, bf16[]{:T(256)} %constant.51.clone.1), kind=kCustom, calls=%fused_computation.6 | custom fusion | bytes 2621952 | tf_op jit(solution)/shard_map/scatter | solution.py:26
  32.6 16.1 %all-to-all-done.2 = bf16[4,320,384]{2,1,0:T(8,128)(2,1)S(1)} async-done(((bf16[4,320,384]{2,1,0:T(8,128)(2,1)}), bf16[4,320,384]{2,1,0:T(8,128)(2,1)S(1)}, u32[]{:S(2)}, u32[]{:S(2)}) %all-to-all-start.2) | async-done | bytes 983072 | tf_op jit(solution)/shard_map/all_to_all | solution.py:35
  48.7 62.7 %all_to_all.15 = bf16[4,320,1024]{2,1,0:T(8,128)(2,1)S(1)} all-to-all(bf16[4,320,1024]{2,1,0:T(8,128)(2,1)} %bitcast.56), channel_id=1, replica_groups=mesh['dp'=8,'expert'=4] {'expert'}, dimensions={0} | all-to-all | bytes 5242880 | tf_op jit(solution)/shard_map/all_to_all | solution.py:34
  111.5 1.2 convert_add_fusion
  112.7 0.3 copy-done.1
  113.0 1.5 fusion.6
  114.5 23.2 %psum.14 = f32[384,32]{0,1:T(8,128)S(1)} all-reduce(f32[384,32]{0,1:T(8,128)S(1)} %fusion.6), channel_id=1, replica_groups=mesh['dp'=8,'expert'=4] {'dp'}, use_global_device_ids=true, to_apply=%region_5.6 | all-reduce | flops 12288 | bytes 98304 | tf_op jit(solution)/shard_map/psum | solution.py:53
  138.0 4.3 %convolution_convert_fusion = bf16[4,320,384]{2,1,0:T(8,128)(2,1)} fusion(bf16[4,320,1024]{2,1,0:T(8,128)(2,1)} %copy-done.1, bf16[1,384,1024]{2,1,0:T(8,128)(2,1)S(1)} %copy-done), kind=kOutput, calls=%fused_computation.5 | convolution fusion | flops 1007124480 | bytes 4390912 | tf_op jit(solution)/shard_map/dot_general | solution.py:37
  142.3 3.6 %all-to-all-start.1 = ((bf16[4,320,384]{2,1,0:T(8,128)(2,1)}), bf16[4,320,384]{2,1,0:T(8,128)(2,1)S(1)}, u32[]{:S(2)}, u32[]{:S(2)}) async-start(bf16[4,320,384]{2,1,0:T(8,128)(2,1)} %convolution_convert_fusion), calls=%async_computation.1 | async-start | bytes 1966080 | tf_op jit(solution)/shard_map/all_to_all | solution.py:40
  146.0 2.9 %cholesky.16 = f32[32,32]{1,0:T(8,128)S(1)} custom-call(f32[32,32]{1,0:T(8,128)S(1)} %fusion.13), custom_call_target="Cholesky" | custom-call | tf_op jit(solution)/shard_map/jit(cholesky)/cholesky | solution.py:14
  149.0 0.6 compare_reduce_fusion
  149.6 0.7 fusion.10
  150.3 2.5 %custom-call.6 = f32[1,32,32]{1,2,0:T(8,128)S(1)} custom-call(f32[1,32,32]{2,1,0:T(8,128)S(1)} %fusion.10), custom_call_target="InvertDiagBlocksLowerTriangular" | custom-call | tf_op jit(solution)/shard_map/triangular_solve | solution.py:15
  153.0 1.7 fusion.19
  154.7 53.3 %all-reduce.2.cloned.1.call-done = f32[1024,32]{0,1:T(8,128)} async-done(((f32[1024,32]{0,1:T(8,128)}), f32[1024,32]{0,1:T(8,128)}) %all-reduce.2.cloned.1.call-update) | async-done | bytes 131088 | tf_op jit(solution)/shard_map/psum | solution.py:57
  208.1 3.3 %fusion.2 = bf16[1,1,384,1024]{3,2,1,0:T(8,128)(2,1)} fusion(f32[384,1024]{1,0:T(8,128)S(1)} %convert_add_fusion, f32[384,32]{0,1:T(8,128)S(1)} %fusion.11, f32[1024,32]{0,1:T(8,128)} %all-reduce.2.cloned.1.call-done), kind=kOutput, calls=%fused_computation.8 | convolution fusion | flops 151814144 | bytes 2539520 | tf_op jit(solution)/shard_map/dot_general | solution.py:58
  211.4 0.7 multiply_bitcast_fusion
  212.0 3.2 %gather_fusion = bf16[640,384]{1,0:T(8,128)(2,1)} fusion(bf16[1280,384]{1,0:T(8,128)(2,1)S(1)} %bitcast.55, s32[1024]{0:T(1024)S(1)} %pad_clamp_fusion), kind=kCustom, calls=%fused_computation | custom fusion | bytes 985600 | tf_op jit(solution)/shard_map/gather | solution.py:49
  (23 shorter events, 1.2 us)
Async XLA Ops:
  7.2 130.8 %copy-start = (bf16[1,384,1024]{2,1,0:T(8,128)(2,1)S(1)}, bf16[1,384,1024]{2,1,0:T(8,128)(2,1)}, u32[]{:S(2)}) copy-start(bf16[1,384,1024]{2,1,0:T(8,128)(2,1)} %param.9) | copy-start | bytes 2359300
  18.1 30.7 %all-to-all-start.2 = ((bf16[4,320,384]{2,1,0:T(8,128)(2,1)}), bf16[4,320,384]{2,1,0:T(8,128)(2,1)S(1)}, u32[]{:S(2)}, u32[]{:S(2)}) async-start(bf16[4,320,384]{2,1,0:T(8,128)(2,1)} %bitcast.6), calls=%async_computation.2 | async-start | bytes 1966080 | tf_op jit(solution)/shard_map/all_to_all | solution.py:35
  48.7 62.8 %copy-start.2 = (bf16[1,1,384,1024]{3,2,1,0:T(8,128)(2,1)S(1)}, bf16[1,1,384,1024]{3,2,1,0:T(8,128)(2,1)}, u32[]{:S(2)}) copy-start(bf16[1,1,384,1024]{3,2,1,0:T(8,128)(2,1)} %param.10) | copy-start | bytes 2359300
  111.5 1.5 copy-start.1
  111.5 1.5 copy-start.5
  142.3 69.8 %all-to-all-start.1 = ((bf16[4,320,384]{2,1,0:T(8,128)(2,1)}), bf16[4,320,384]{2,1,0:T(8,128)(2,1)S(1)}, u32[]{:S(2)}, u32[]{:S(2)}) async-start(bf16[4,320,384]{2,1,0:T(8,128)(2,1)} %convolution_convert_fusion), calls=%async_computation.1 | async-start | bytes 1966080 | tf_op jit(solution)/shard_map/all_to_all | solution.py:40
  145.8 62.2 %all-reduce.2.cloned.1.call-start = ((), (), s32[]{:S(2)}) async-start(), calls=%async_computation.3 | async-start | bytes 262144 | tf_op jit(solution)/shard_map/psum | solution.py:57
  153.0 58.4 %copy-start.4 = (f32[384,32]{0,1:T(8,128)}, f32[384,32]{0,1:T(8,128)S(1)}, u32[]{:S(2)}) copy-start(f32[384,32]{0,1:T(8,128)S(1)} %fusion.11) | copy-start | bytes 147460
  208.1 3.3 %copy-start.3 = (f32[1024,32]{0,1:T(8,128)S(1)}, f32[1024,32]{0,1:T(8,128)}, u32[]{:S(2)}) copy-start(f32[1024,32]{0,1:T(8,128)} %all-reduce.2.cloned.1.call-done) | copy-start | bytes 393220
Sparse Core Ops, SparseCore 0:
  154.8 53.1 all-reduce.1
where the time goes:
time: 223 us; the launch traced here: 222 us
  blocking collectives  86 us (39%)
  waiting for transfers between devices  69.4 us (31%)
  local copies, waits for them, and re-layouts  19.1 us (9%)
  between operations  14.1 us (6%)
  matrix products  12.4 us (6%)
  other arithmetic  10.9 us (5%)
  starting transfers between devices  10.1 us (5%)
    all_to_all x1, blocking collectives, shards(): lax.all_to_all(grad_buffer, 'expert', split_axis=0, concat_axis=0, tiled=...  62.7 us
    psum x1, waiting for transfers between devices, shards(): right_factor = lax.psum(right_local, 'dp') / lax.axis_size('dp')  53.3 us
    psum x1, blocking collectives, shards(): left_sum = lax.psum(left_local, 'dp')  23.2 us
    all_to_all x1, waiting for transfers between devices, shards(): lax.all_to_all(hidden_buffer, 'expert', split_axis=0, concat_axis=0, tile...  16.1 us
    scatter x1, local copies, waits for them, and re-layouts, shards(): jnp.zeros((experts * capacity, width), jnp.bfloat16).at[slot_index]  8.24 us
    scatter x1, local copies, waits for them, and re-layouts, shards(): jnp.zeros((experts * capacity, hidden_width), jnp.bfloat16).at[slot_index]  7.1 us
    all_to_all x1, starting transfers between devices, shards(): lax.all_to_all(hidden_buffer, 'expert', split_axis=0, concat_axis=0, tile...  6.35 us
  transfers between devices with their start and end apart: 3, of which 2 were waited for; matrix products, arithmetic and copies ran while one was open for 9% of the time, Pallas kernels for 0%

commit v1 on v0

v1 whole, which is shorter than its diff:
```python
import jax
import jax.numpy as jnp
from jax import lax
from jax.experimental import pallas as pl
from jax.experimental.pallas import tpu as pltpu
from jax.sharding import PartitionSpec as P

HIGHEST = lax.Precision.HIGHEST
F32 = jnp.float32
BF16 = jnp.bfloat16


def bits_of(size):
    return [1 << i for i in range(size.bit_length() - 1)]


def swap(value, axis, bit):
    size = lax.axis_size(axis)
    return lax.ppermute(value, axis, [(i, i ^ bit) for i in range(size)])


def shift(value, axis, step):
    size = lax.axis_size(axis)
    return lax.ppermute(value, axis, [(i, (i + step) % size) for i in range(size)])


def has_bit(bit):
    return (lax.axis_index("dp") & bit) != 0


def scatter_sum(value):
    for bit in bits_of(lax.axis_size("dp")):
        half = value.shape[0] // 2
        low, high = value[:half], value[half:]
        mine = has_bit(bit)
        sent = jnp.where(mine, low, high)
        kept = jnp.where(mine, high, low)
        value = kept + swap(sent, "dp", bit)
    return value


def gather_rows(value):
    for bit in reversed(bits_of(lax.axis_size("dp"))):
        other = swap(value, "dp", bit)
        mine = has_bit(bit)
        value = jnp.concatenate([jnp.where(mine, other, value), jnp.where(mine, value, other)], axis=0)
    return value


def own_block(value):
    size = lax.axis_size("dp")
    index = jnp.int32(0)
    for bit in bits_of(size):
        index = index * 2 + has_bit(bit).astype(jnp.int32)
    rows = value.shape[0] // size
    return lax.dynamic_slice_in_dim(value, index * rows, rows, 0)


def after(value, *others):
    return lax.optimization_barrier((value,) + others)[0]


def pack_kernel(experts, capacity, steps, rel_ref, grad_ref, hidden_ref, *out_refs):
    rows = grad_ref.shape[0]
    width = grad_ref.shape[1]
    rel = rel_ref[...]
    group = lax.broadcasted_iota(jnp.int32, (experts, rows), 0)
    onehot = (group == rel).astype(F32)
    before = (
        lax.broadcasted_iota(jnp.int32, (rows, rows), 0) < lax.broadcasted_iota(jnp.int32, (rows, rows), 1)
    ).astype(F32).astype(BF16)
    ranks = jnp.dot(onehot.astype(BF16), before, preferred_element_type=F32)
    rank = jnp.sum(ranks * onehot, axis=0, keepdims=True).astype(jnp.int32)
    slot = lax.broadcasted_iota(jnp.int32, (capacity, rows), 0)
    for step, out_ref in zip(steps, out_refs):
        target = jnp.where(rel == step, rank, -1)
        pick = (slot == target).astype(F32).astype(BF16)
        out_ref[:, :width] = jnp.dot(pick, grad_ref[...], preferred_element_type=F32).astype(BF16)
        out_ref[:, width:] = jnp.dot(pick, hidden_ref[...], preferred_element_type=F32).astype(BF16)


def pack(rel, grad_out, hidden_acts, capacity, steps):
    experts = lax.axis_size("expert")
    row_count, width = grad_out.shape
    total = width + hidden_acts.shape[1]
    return pl.pallas_call(
        lambda *refs: pack_kernel(experts, capacity, steps, *refs),
        out_shape=[jax.ShapeDtypeStruct((capacity, total), BF16) for _ in steps],
        name="pack_rows",
    )(rel.reshape(1, row_count), grad_out, hidden_acts)


def pad_lanes(value, lanes):
    return jnp.pad(value, ((0, 0), (0, lanes - value.shape[1])))


def shards(grad_out, hidden_acts, expert_ids, down_weight, error_in, q_prev):
    experts = lax.axis_size("expert")
    replicas = lax.axis_size("dp")
    place = lax.axis_index("expert")
    row_count, width = grad_out.shape
    hidden_width = hidden_acts.shape[1]
    capacity = 2 * row_count // experts
    rank = q_prev.shape[2]
    lanes = experts * rank
    rel = lax.rem(place - expert_ids + experts, experts)
    weight, q_own, error = down_weight[0], q_prev[0], error_in[0, 0]

    steps = list(range(1, experts))
    q_block = own_block(q_own)
    q_blocks = jnp.concatenate([q_block] + [shift(q_block, "expert", k) for k in steps], axis=1)
    weight_block = own_block(weight)
    weight_blocks = [shift(weight_block, "expert", k) for k in steps]
    packed_first = pack(rel, grad_out, hidden_acts, capacity, steps[:1])
    packed_rest = pack(rel, grad_out, hidden_acts, capacity, steps[1:])
    recv = [shift(packed_first[0], "expert", -1)]

    group = lax.broadcasted_iota(jnp.int32, (row_count, lanes), 1) // rank
    chosen = (group == rel[:, None]).astype(F32)
    error_f = error.astype(F32)
    grad_f = grad_out.astype(F32)
    hidden_f = hidden_acts.astype(F32)

    q_all = gather_rows(q_blocks)
    row_q = jnp.dot(grad_f, q_all, precision=HIGHEST) * chosen
    left_part = lax.dot_general(hidden_f, row_q, (((0,), (0,)), ((), ())), precision=HIGHEST)
    left_part = left_part + pad_lanes(jnp.dot(error_f, q_own, precision=HIGHEST), lanes)
    left_block = scatter_sum(left_part)
    left_recv = [shift(left_block, "expert", k) for k in steps]
    left_block_sum = left_block
    for k in steps:
        left_block_sum = left_block_sum + jnp.roll(left_recv[k - 1], k * rank, axis=1)
    left_sum = gather_rows(left_block_sum)

    packed_rest = [after(p, *left_recv) for p in packed_rest]
    recv += [shift(p, "expert", -k) for k, p in zip(steps[1:], packed_rest)]

    left_each = left_sum.reshape(hidden_width, experts, rank).transpose(1, 0, 2)
    gram = jnp.einsum("efr,efs->ers", left_each, left_each, precision=HIGHEST)
    chol = jnp.linalg.cholesky(gram)
    left_factors = lax.linalg.triangular_solve(chol, left_each, left_side=False, lower=True, transpose_a=True)
    left_own = left_factors[0]
    left_all = left_factors.transpose(1, 0, 2).reshape(hidden_width, lanes)

    row_l = jnp.dot(hidden_f, left_all, precision=HIGHEST) * chosen
    right_part = lax.dot_general(grad_f, row_l, (((0,), (0,)), ((), ())), precision=HIGHEST)
    right_part = right_part + pad_lanes(
        lax.dot_general(error_f, left_own, (((0,), (0,)), ((), ())), precision=HIGHEST), lanes
    )
    right_block = scatter_sum(right_part)
    right_recv = [shift(right_block[:, k * rank : (k + 1) * rank], "expert", -k) for k in steps]
    right_own = right_block[:, :rank]
    for r in right_recv:
        right_own = right_own + r
    right_factor = gather_rows(right_own) / replicas

    own_weight_block = weight_block
    blocks = jnp.concatenate([b[:, None] for b in weight_blocks], axis=1)
    blocks = after(blocks, left_sum)
    others = gather_rows(blocks)
    grad_hidden = lax.dot_general(grad_out, weight, (((1,), (1,)), ((), ())), preferred_element_type=F32)
    for k in steps:
        product = lax.dot_general(
            grad_out, others[:, k - 1], (((1,), (1,)), ((), ())), preferred_element_type=F32
        )
        grad_hidden = jnp.where((rel == k)[:, None], product, grad_hidden)
    grad_hidden = grad_hidden.astype(BF16)

    own_hidden = jnp.where((rel == 0)[:, None], hidden_acts, jnp.zeros((), BF16))
    rows_product = lambda h, g: lax.dot_general(h, g, (((0,), (0,)), ((), ())), preferred_element_type=F32)
    merged = error_f + rows_product(own_hidden, grad_out)
    for r in recv:
        merged = merged + rows_product(r[:, width:], r[:, :width])
    approx = lax.dot_general(left_own, right_factor, (((1,), (1,)), ((), ())), precision=HIGHEST)
    error_out = (merged - approx).astype(BF16)
    return (grad_hidden, left_own[None], right_factor[None], error_out[None, None])


def solution(mesh):
    placed = (
        P(("dp", "expert"), None),
        P(("dp", "expert"), None),
        P(("dp", "expert")),
        P("expert", None, None),
        P("dp", "expert", None, None),
        P("expert", None, None),
    )
    return jax.shard_map(
        shards,
        mesh=mesh,
        in_specs=placed,
        out_specs=(
            P(("dp", "expert"), None),
            P("expert", None, None),
            P("expert", None, None),
            P("dp", "expert", None, None),
        ),
        check_vma=False,
    )
```

time: 223 us -> 175 us (0.78)
  blocking collectives: 86 us -> 0 us
  starting transfers between devices: 10.1 us -> 39.5 us
  other arithmetic: 10.9 us -> 28.1 us
  between operations: 14.1 us -> 1.22 us
  local copies, waits for them, and re-layouts: 19.1 us -> 7.99 us
  Pallas kernels: 0 us -> 7.86 us
  matrix products: 12.4 us -> 17.9 us
    ppermute x0 -> x33, waiting for transfers between devices: none -> 71.6 us  [the longest x18 38.1 us: swap(): return lax.ppermute(value, axis, [(i, i ^ bit) for i in range(size)])]
    all_to_all x1 -> x0, blocking collectives: 62.7 us -> none  [shards(): lax.all_to_all(grad_buffer, 'expert', split_axis=0, concat_axis=0, tiled=...]
    psum x1 -> x0, waiting for transfers between devices: 53.3 us -> none  [shards(): right_factor = lax.psum(right_local, 'dp') / lax.axis_size('dp')]
    ppermute x0 -> x33, starting transfers between devices: none -> 39.5 us  [the longest x15 25 us: shift(): lax.ppermute(value, axis, [(i, (i + step) % size) for i in range(size)])]
    psum x1 -> x0, blocking collectives: 23.2 us -> none  [shards(): left_sum = lax.psum(left_local, 'dp')]
    all_to_all x2 -> x0, waiting for transfers between devices: 16.1 us -> none  [the longest x1 16.1 us: shards(): lax.all_to_all(hidden_buffer, 'expert', split_axis=0, concat_axis=0, tile...]
    scatter x2 -> x0, local copies, waits for them, and re-layouts: 15.3 us -> none  [the longest x1 8.24 us: shards(): jnp.zeros((experts * capacity, width), jnp.bfloat16).at[slot_index]]
    another operation x7, other arithmetic: 8.01 us -> 23.1 us  [the longest x4 11.9 us: shards(): chol = jnp.linalg.cholesky(gram)]
  transfers between devices with their start and end apart: 3 -> 33, of which waited for: 2 -> 20; matrix products, arithmetic and copies ran while one was open for 9% -> 26% of each run, Pallas kernels for 0% -> 5%
where the time goes in v1:
time: 175 us; the launch traced here: 174 us
  waiting for transfers between devices  71.6 us (41%)
  starting transfers between devices  39.5 us (23%)
  other arithmetic  28.1 us (16%)
  matrix products  17.9 us (10%)
  local copies, waits for them, and re-layouts  7.99 us (5%)
  Pallas kernels  7.86 us (4%)
    ppermute x18, waiting for transfers between devices, swap(): return lax.ppermute(value, axis, [(i, i ^ bit) for i in range(size)])  38.1 us
    ppermute x15, waiting for transfers between devices, shift(): lax.ppermute(value, axis, [(i, (i + step) % size) for i in range(size)])  33.5 us
    ppermute x15, starting transfers between devices, shift(): lax.ppermute(value, axis, [(i, (i + step) % size) for i in range(size)])  25 us
    ppermute x18, starting transfers between devices, swap(): return lax.ppermute(value, axis, [(i, i ^ bit) for i in range(size)])  14.5 us
    another operation x4, other arithmetic, shards(): chol = jnp.linalg.cholesky(gram)  11.9 us
    another operation x3, other arithmetic, shards(): lax.linalg.triangular_solve(chol, left_each, left_side=False, lower=True,...  11.3 us
    pallas_call x2, Pallas kernels, pack(): pl.pallas_call(lambda *refs: pack_kernel(experts, capacity, steps, *refs)...  7.86 us
    dot_general x4, matrix products, shards(): lax.dot_general(h, g, (((0,), (0,)), ((), ())), preferred_element_type=F32)  5.06 us
  transfers between devices with their start and end apart: 33, of which 20 were waited for; matrix products, arithmetic and copies ran while one was open for 26% of the time, Pallas kernels for 5%

profile of v1, /device:TPU:0, one launch (start us, length us, event | category | flops | bytes accessed | tf_op | source)
XLA Modules:
  0.0 174.1 jit_solution(7102019298631232837)
XLA Ops:
  1.5 3.1 %collective-permute-start.3 = (f32[128,32]{0,1:T(8,128)S(1)}, f32[128,32]{0,1:T(8,128)S(1)}, u32[]{:S(2)}, u32[]{:S(2)}) collective-permute-start(f32[128,32]{0,1:T(8,128)S(1)} %dynamic-slice_bitcast_fusion.1), channel_id=1, source_target_pairs={{0,1},{1,2},{2,3},{3,0},{4,5},{5,6},{6,7},{7,4},{8,9},{9,10},{10,1... | collective-permute-start | bytes 49160 | tf_op jit(solution)/shard_map/ppermute | solution.py:24
  4.6 2.6 %collective-permute-start.4 = (f32[128,32]{0,1:T(8,128)S(1)}, f32[128,32]{0,1:T(8,128)S(1)}, u32[]{:S(2)}, u32[]{:S(2)}) collective-permute-start(f32[128,32]{0,1:T(8,128)S(1)} %dynamic-slice_bitcast_fusion.1), channel_id=1, source_target_pairs={{0,2},{1,3},{2,0},{3,1},{4,6},{5,7},{6,4},{7,5},{8,10},{9,11},{10,... | collective-permute-start | bytes 49160 | tf_op jit(solution)/shard_map/ppermute | solution.py:24
  9.3 1.6 collective-permute-done.5
  12.4 2.7 %collective-permute-done.6 = f32[128,128]{0,1:T(8,128)S(1)} collective-permute-done((f32[128,128]{0,1:T(8,128)S(1)}, f32[128,128]{0,1:T(8,128)S(1)}, u32[]{:S(2)}, u32[]{:S(2)}) %collective-permute-start.6) | collective-permute-done | bytes 65568 | tf_op jit(solution)/shard_map/ppermute | solution.py:19
  17.5 2.8 %collective-permute-done.7 = f32[256,128]{0,1:T(8,128)S(1)} collective-permute-done((f32[256,128]{0,1:T(8,128)S(1)}, f32[256,128]{0,1:T(8,128)S(1)}, u32[]{:S(2)}, u32[]{:S(2)}) %collective-permute-start.7) | collective-permute-done | bytes 131104 | tf_op jit(solution)/shard_map/ppermute | solution.py:19
  27.0 2.8 %collective-permute-done.10 = f32[96,128]{0,1:T(8,128)S(1)} collective-permute-done((f32[96,128]{0,1:T(8,128)S(1)}, f32[96,128]{0,1:T(8,128)S(1)}, u32[]{:S(2)}, u32[]{:S(2)}) %collective-permute-start.10) | collective-permute-done | bytes 49184 | tf_op jit(solution)/shard_map/ppermute | solution.py:19
  31.6 2.7 %collective-permute-done.11 = f32[48,128]{0,1:T(8,128)S(1)} collective-permute-done((f32[48,128]{0,1:T(8,128)S(1)}, f32[48,128]{0,1:T(8,128)S(1)}, u32[]{:S(2)}, u32[]{:S(2)}) %collective-permute-start.11) | collective-permute-done | bytes 24608 | tf_op jit(solution)/shard_map/ppermute | solution.py:19
  35.5 2.7 %collective-permute-start.12 = (f32[48,128]{0,1:T(8,128)S(1)}, f32[48,128]{0,1:T(8,128)}, u32[]{:S(2)}, u32[]{:S(2)}) collective-permute-start(f32[48,128]{0,1:T(8,128)S(1)} %select_add_fusion.4), channel_id=1, source_target_pairs={{0,1},{1,2},{2,3},{3,0},{4,5},{5,6},{6,7},{7,4},{8,9},{9,10},{10,1... | collective-permute-start | bytes 73736 | tf_op jit(solution)/shard_map/ppermute | solution.py:24
  41.5 3.6 %pack_rows.2 = bf16[320,1408]{1,0:T(8,128)(2,1)} custom-call(s32[1,640]{1,0:T(1,128)} %reshape.66.refs_0_, bf16[640,1024]{1,0:T(8,128)(2,1)} %refs_1_.3, bf16[640,384]{1,0:T(8,128)(2,1)} %refs_2_.3), custom_call_target="tpu_custom_call" | custom-call | tf_op jit(solution)/shard_map/pack_rows/pallas_call | solution.py:86
  45.2 2.8 %collective-permute-start.2 = (bf16[48,1024]{1,0:T(8,128)(2,1)}, bf16[48,1024]{1,0:T(8,128)(2,1)}, u32[]{:S(2)}, u32[]{:S(2)}) collective-permute-start(bf16[48,1024]{1,0:T(8,128)(2,1)} %dynamic-slice_bitcast_fusion), channel_id=1, source_target_pairs={{0,3},{1,0},{2,1},{3,2},{4,7},{5,4},{6,5},{7,6},{8,11},{9,8},{10,9... | collective-permute-start | bytes 294920 | tf_op jit(solution)/shard_map/ppermute | solution.py:24
  54.9 2.1 %fusion.32 = f32[384,1024]{1,0:T(8,128)} fusion(bf16[640,1024]{1,0:T(8,128)(2,1)S(1)} %copy-done.2, bf16[640,384]{1,0:T(8,128)(2,1)S(1)} %copy-done.5, pred[640]{0:T(1024)(128)(4,1)S(1)} %get-tuple-element.26), kind=kOutput, calls=%fused_computation.49 | convolution fusion | flops 503562240 | bytes 3375744 | tf_op jit(solution)/shard_map/dot_general | solution.py:170
  59.3 4.2 %pack_rows.3 = (bf16[320,1408]{1,0:T(8,128)(2,1)}, bf16[320,1408]{1,0:T(8,128)(2,1)}) custom-call(s32[1,640]{1,0:T(1,128)} %reshape.66.refs_0_, bf16[640,1024]{1,0:T(8,128)(2,1)} %refs_1_.3, bf16[640,384]{1,0:T(8,128)(2,1)} %refs_2_.3), custom_call_target="tpu_custom_call" | custom-call | tf_op jit(solution)/shard_map/pack_rows/pallas_call | solution.py:86
  66.5 11.7 %custom-call.7 = f32[4,32,32]{2,1,0:T(8,128)S(1)} custom-call(f32[4,32,32]{2,1,0:T(8,128)S(1)} %fusion.47), custom_call_target="Cholesky" | custom-call | tf_op jit(solution)/shard_map/jit(cholesky)/cholesky | solution.py:140
  79.1 10.5 %custom-call.8 = f32[4,1,32,32]{2,3,1,0:T(8,128)S(1)} custom-call(f32[4,1,32,32]{3,2,1,0:T(8,128)} %select_bitcast_fusion), custom_call_target="InvertDiagBlocksLowerTriangular" | custom-call | tf_op jit(solution)/shard_map/triangular_solve | solution.py:141
  96.0 5.0 %collective-permute-done.22 = f32[256,128]{0,1:T(8,128)S(1)} collective-permute-done((f32[256,128]{0,1:T(8,128)S(1)}, f32[256,128]{0,1:T(8,128)S(1)}, u32[]{:S(2)}, u32[]{:S(2)}) %collective-permute-start.22) | collective-permute-done | bytes 131104 | tf_op jit(solution)/shard_map/ppermute | solution.py:19
  105.4 2.7 %collective-permute-start.24 = (f32[128,32]{0,1:T(8,128)S(1)}, f32[128,32]{0,1:T(8,128)S(1)}, u32[]{:S(2)}, u32[]{:S(2)}) collective-permute-start(f32[128,32]{0,1:T(8,128)S(1)} %get-tuple-element.50), channel_id=1, source_target_pairs={{0,3},{1,0},{2,1},{3,2},{4,7},{5,4},{6,5},{7,6},{8,11},{9,8},{10,9... | collective-permute-start | bytes 49160 | tf_op jit(solution)/shard_map/ppermute | solution.py:24
  108.1 3.7 %collective-permute-done.18 = bf16[48,3,1024]{2,0,1:T(8,128)(2,1)S(1)} collective-permute-done((bf16[48,3,1024]{2,0,1:T(8,128)(2,1)S(1)}, bf16[48,3,1024]{2,0,1:T(8,128)(2,1)S(1)}, u32[]{:S(2)}, u32[]{:S(2)}) %collective-permute-start.18) | collective-permute-done | bytes 294944 | tf_op jit(solution)/shard_map/ppermute | solution.py:19
  112.5 12.4 %collective-permute-done.24 = f32[128,32]{0,1:T(8,128)S(1)} collective-permute-done((f32[128,32]{0,1:T(8,128)S(1)}, f32[128,32]{0,1:T(8,128)S(1)}, u32[]{:S(2)}, u32[]{:S(2)}) %collective-permute-start.24) | collective-permute-done | bytes 16416 | tf_op jit(solution)/shard_map/ppermute | solution.py:24
  124.9 4.0 %collective-permute-start.31 = (bf16[320,1408]{1,0:T(8,128)(2,1)S(1)}, bf16[320,1408]{1,0:T(8,128)(2,1)S(1)}, u32[]{:S(2)}, u32[]{:S(2)}) collective-permute-start(bf16[320,1408]{1,0:T(8,128)(2,1)S(1)} %copy-done.13), channel_id=1, source_target_pairs={{0,2},{1,3},{2,0},{3,1},{4,6},{5,7},{6,4},{7,5},{8,10},{9,11},{10,... | collective-permute-start | bytes 2703368 | tf_op jit(solution)/shard_map/ppermute | solution.py:24
  128.9 18.2 %collective-permute-done.25 = f32[128,32]{0,1:T(8,128)S(1)} collective-permute-done((f32[128,32]{0,1:T(8,128)S(1)}, f32[128,32]{0,1:T(8,128)S(1)}, u32[]{:S(2)}, u32[]{:S(2)}) %collective-permute-start.25) | collective-permute-done | bytes 16416 | tf_op jit(solution)/shard_map/ppermute | solution.py:24
  147.8 3.1 %collective-permute-done.27 = f32[128,32]{0,1:T(8,128)S(1)} collective-permute-done((f32[128,32]{0,1:T(8,128)S(1)}, f32[128,32]{0,1:T(8,128)S(1)}, u32[]{:S(2)}, u32[]{:S(2)}) %collective-permute-start.27) | collective-permute-done | bytes 16416 | tf_op jit(solution)/shard_map/ppermute | solution.py:19
  151.5 1.8 %fusion.27 = f32[384,1024]{1,0:T(8,128)S(1)} fusion(bf16[320,1408]{1,0:T(8,128)(2,1)} %collective-permute-done.30), kind=kOutput, calls=%fused_computation.41 | convolution fusion | flops 251658240 | bytes 2473984 | tf_op jit(solution)/shard_map/dot_general | solution.py:170
  153.3 9.8 %collective-permute-done.28 = f32[256,32]{0,1:T(8,128)S(1)} collective-permute-done((f32[256,32]{0,1:T(8,128)S(1)}, f32[256,32]{0,1:T(8,128)S(1)}, u32[]{:S(2)}, u32[]{:S(2)}) %collective-permute-start.28) | collective-permute-done | bytes 32800 | tf_op jit(solution)/shard_map/ppermute | solution.py:19
  167.1 2.8 %fusion.8 = bf16[1,1,384,1024]{3,2,1,0:T(8,128)(2,1)} fusion(f32[384,1024]{1,0:T(8,128)S(1)} %fusion.23, f32[384,1024]{1,0:T(8,128)S(1)} %fusion.25, f32[384,1024]{1,0:T(8,128)S(1)} %fusion.27, f32[384,1024]{1,0:T(8,128)S(1)} %copy-done.7, bf16[1,1,384,1024]{3,2,1,0:T(8,128)(2,1)S(1)} %copy-done.8, f32[512,32]{0,1:T(8,128)S(1)} %get-tuple-element.41, ...), kind=kOutput, calls=%fused_computation.24 | convolution fusion | flops 153812992 | bytes 8044544 | tf_op jit(solution)/shard_map/dot_general | solution.py:174
  (153 shorter events, 53.4 us)
Async XLA Ops:
  1.5 7.0 %collective-permute-start.3 = (f32[128,32]{0,1:T(8,128)S(1)}, f32[128,32]{0,1:T(8,128)S(1)}, u32[]{:S(2)}, u32[]{:S(2)}) collective-permute-start(f32[128,32]{0,1:T(8,128)S(1)} %dynamic-slice_bitcast_fusion.1), channel_id=1, source_target_pairs={{0,1},{1,2},{2,3},{3,0},{4,5},{5,6},{6,7},{7,4},{8,9},{9,10},{10,1... | collective-permute-start | bytes 49160 | tf_op jit(solution)/shard_map/ppermute | solution.py:24
  4.6 4.7 %collective-permute-start.4 = (f32[128,32]{0,1:T(8,128)S(1)}, f32[128,32]{0,1:T(8,128)S(1)}, u32[]{:S(2)}, u32[]{:S(2)}) collective-permute-start(f32[128,32]{0,1:T(8,128)S(1)} %dynamic-slice_bitcast_fusion.1), channel_id=1, source_target_pairs={{0,2},{1,3},{2,0},{3,1},{4,6},{5,7},{6,4},{7,5},{8,10},{9,11},{10,... | collective-permute-start | bytes 49160 | tf_op jit(solution)/shard_map/ppermute | solution.py:24
  15.2 5.0 %collective-permute-start.7 = (f32[256,128]{0,1:T(8,128)S(1)}, f32[256,128]{0,1:T(8,128)S(1)}, u32[]{:S(2)}, u32[]{:S(2)}) collective-permute-start(f32[256,128]{0,1:T(8,128)S(1)} %pad_maximum_fusion.6), channel_id=1, source_target_pairs={{0,8},{4,12},{8,0},{12,4},{16,24},{20,28},{24,16},{28,20},{1,9},{5... | collective-permute-start | bytes 393224 | tf_op jit(solution)/shard_map/ppermute | solution.py:19
  25.5 4.3 %collective-permute-start.10 = (f32[96,128]{0,1:T(8,128)S(1)}, f32[96,128]{0,1:T(8,128)S(1)}, u32[]{:S(2)}, u32[]{:S(2)}) collective-permute-start(f32[96,128]{0,1:T(8,128)S(1)} %slice_select_fusion.5), channel_id=1, source_target_pairs={{0,8},{4,12},{8,0},{12,4},{16,24},{20,28},{24,16},{28,20},{1,9},{5... | collective-permute-start | bytes 147464 | tf_op jit(solution)/shard_map/ppermute | solution.py:19
  30.0 4.3 %collective-permute-start.11 = (f32[48,128]{0,1:T(8,128)S(1)}, f32[48,128]{0,1:T(8,128)S(1)}, u32[]{:S(2)}, u32[]{:S(2)}) collective-permute-start(f32[48,128]{0,1:T(8,128)S(1)} %slice_select_fusion.4), channel_id=1, source_target_pairs={{0,16},{4,20},{8,24},{12,28},{16,0},{20,4},{24,8},{28,12},{1,17},{... | collective-permute-start | bytes 73736 | tf_op jit(solution)/shard_map/ppermute | solution.py:19
  34.4 18.1 %collective-permute-start.13 = (f32[48,128]{0,1:T(8,128)S(1)}, f32[48,128]{0,1:T(8,128)}, u32[]{:S(2)}, u32[]{:S(2)}) collective-permute-start(f32[48,128]{0,1:T(8,128)S(1)} %select_add_fusion.4), channel_id=1, source_target_pairs={{0,2},{1,3},{2,0},{3,1},{4,6},{5,7},{6,4},{7,5},{8,10},{9,11},{10,... | collective-permute-start | bytes 73736 | tf_op jit(solution)/shard_map/ppermute | solution.py:24
  35.5 9.7 %collective-permute-start.12 = (f32[48,128]{0,1:T(8,128)S(1)}, f32[48,128]{0,1:T(8,128)}, u32[]{:S(2)}, u32[]{:S(2)}) collective-permute-start(f32[48,128]{0,1:T(8,128)S(1)} %select_add_fusion.4), channel_id=1, source_target_pairs={{0,1},{1,2},{2,3},{3,0},{4,5},{5,6},{6,7},{7,4},{8,9},{9,10},{10,1... | collective-permute-start | bytes 73736 | tf_op jit(solution)/shard_map/ppermute | solution.py:24
  38.2 11.3 %collective-permute-start.14 = (f32[48,128]{0,1:T(8,128)S(1)}, f32[48,128]{0,1:T(8,128)}, u32[]{:S(2)}, u32[]{:S(2)}) collective-permute-start(f32[48,128]{0,1:T(8,128)S(1)} %select_add_fusion.4), channel_id=1, source_target_pairs={{0,3},{1,0},{2,1},{3,2},{4,7},{5,4},{6,5},{7,6},{8,11},{9,8},{10,9... | collective-permute-start | bytes 73736 | tf_op jit(solution)/shard_map/ppermute | solution.py:24
  39.9 62.7 %collective-permute-start = (bf16[48,1024]{1,0:T(8,128)(2,1)}, bf16[48,1024]{1,0:T(8,128)(2,1)S(1)}, u32[]{:S(2)}, u32[]{:S(2)}) collective-permute-start(bf16[48,1024]{1,0:T(8,128)(2,1)} %dynamic-slice_bitcast_fusion), channel_id=1, source_target_pairs={{0,1},{1,2},{2,3},{3,0},{4,5},{5,6},{6,7},{7,4},{8,9},{9,10},{10,1... | collective-permute-start | bytes 294920 | tf_op jit(solution)/shard_map/ppermute | solution.py:24
  40.9 61.8 %collective-permute-start.1 = (bf16[48,1024]{1,0:T(8,128)(2,1)}, bf16[48,1024]{1,0:T(8,128)(2,1)}, u32[]{:S(2)}, u32[]{:S(2)}) collective-permute-start(bf16[48,1024]{1,0:T(8,128)(2,1)} %dynamic-slice_bitcast_fusion), channel_id=1, source_target_pairs={{0,2},{1,3},{2,0},{3,1},{4,6},{5,7},{6,4},{7,5},{8,10},{9,11},{10,... | collective-permute-start | bytes 294920 | tf_op jit(solution)/shard_map/ppermute | solution.py:24
  45.2 57.5 %collective-permute-start.2 = (bf16[48,1024]{1,0:T(8,128)(2,1)}, bf16[48,1024]{1,0:T(8,128)(2,1)}, u32[]{:S(2)}, u32[]{:S(2)}) collective-permute-start(bf16[48,1024]{1,0:T(8,128)(2,1)} %dynamic-slice_bitcast_fusion), channel_id=1, source_target_pairs={{0,3},{1,0},{2,1},{3,2},{4,7},{5,4},{6,5},{7,6},{8,11},{9,8},{10,9... | collective-permute-start | bytes 294920 | tf_op jit(solution)/shard_map/ppermute | solution.py:24
  49.5 102.0 %collective-permute-start.30 = (bf16[320,1408]{1,0:T(8,128)(2,1)}, bf16[320,1408]{1,0:T(8,128)(2,1)}, u32[]{:S(2)}, u32[]{:S(2)}) collective-permute-start(bf16[320,1408]{1,0:T(8,128)(2,1)} %pack_rows.2), channel_id=1, source_target_pairs={{0,3},{1,0},{2,1},{3,2},{4,7},{5,4},{6,5},{7,6},{8,11},{9,8},{10,9... | collective-permute-start | bytes 2703368 | tf_op jit(solution)/shard_map/ppermute | solution.py:24
  53.3 4.3 %collective-permute-start.15 = (f32[48,128]{0,1:T(8,128)S(1)}, f32[48,128]{0,1:T(8,128)S(1)}, u32[]{:S(2)}, u32[]{:S(2)}) collective-permute-start(f32[48,128]{0,1:T(8,128)S(1)} %fusion.44), channel_id=1, source_target_pairs={{0,16},{4,20},{8,24},{12,28},{16,0},{20,4},{24,8},{28,12},{1,17},{... | collective-permute-start | bytes 73736 | tf_op jit(solution)/shard_map/ppermute | solution.py:19
  57.8 5.8 %collective-permute-start.16 = (f32[96,128]{0,1:T(8,128)S(1)}, f32[96,128]{0,1:T(8,128)S(1)}, u32[]{:S(2)}, u32[]{:S(2)}) collective-permute-start(f32[96,128]{0,1:T(8,128)S(1)} %pad_maximum_fusion.9), channel_id=1, source_target_pairs={{0,8},{4,12},{8,0},{12,4},{16,24},{20,28},{24,16},{28,20},{1,9},{5... | collective-permute-start | bytes 147464 | tf_op jit(solution)/shard_map/ppermute | solution.py:19
  95.4 5.6 %collective-permute-start.22 = (f32[256,128]{0,1:T(8,128)S(1)}, f32[256,128]{0,1:T(8,128)S(1)}, u32[]{:S(2)}, u32[]{:S(2)}) collective-permute-start(f32[256,128]{0,1:T(8,128)S(1)} %slice_select_fusion.1), channel_id=1, source_target_pairs={{0,8},{4,12},{8,0},{12,4},{16,24},{20,28},{24,16},{28,20},{1,9},{5... | collective-permute-start | bytes 393224 | tf_op jit(solution)/shard_map/ppermute | solution.py:19
  103.6 61.5 %collective-permute-start.32 = (bf16[320,1408]{1,0:T(8,128)(2,1)S(1)}, bf16[320,1408]{1,0:T(8,128)(2,1)S(1)}, u32[]{:S(2)}, u32[]{:S(2)}) collective-permute-start(bf16[320,1408]{1,0:T(8,128)(2,1)S(1)} %copy-done.14), channel_id=1, source_target_pairs={{0,1},{1,2},{2,3},{3,0},{4,5},{5,6},{6,7},{7,4},{8,9},{9,10},{10,1... | collective-permute-start | bytes 2703368 | tf_op jit(solution)/shard_map/ppermute | solution.py:24
  104.2 7.6 %collective-permute-start.18 = (bf16[48,3,1024]{2,0,1:T(8,128)(2,1)S(1)}, bf16[48,3,1024]{2,0,1:T(8,128)(2,1)S(1)}, u32[]{:S(2)}, u32[]{:S(2)}) collective-permute-start(bf16[48,3,1024]{2,0,1:T(8,128)(2,1)S(1)} %pad_maximum_fusion.3), channel_id=1, source_target_pairs={{0,16},{4,20},{8,24},{12,28},{16,0},{20,4},{24,8},{28,12},{1,17},{... | collective-permute-start | bytes 884744 | tf_op jit(solution)/shard_map/ppermute | solution.py:19
  105.4 19.5 %collective-permute-start.24 = (f32[128,32]{0,1:T(8,128)S(1)}, f32[128,32]{0,1:T(8,128)S(1)}, u32[]{:S(2)}, u32[]{:S(2)}) collective-permute-start(f32[128,32]{0,1:T(8,128)S(1)} %get-tuple-element.50), channel_id=1, source_target_pairs={{0,3},{1,0},{2,1},{3,2},{4,7},{5,4},{6,5},{7,6},{8,11},{9,8},{10,9... | collective-permute-start | bytes 49160 | tf_op jit(solution)/shard_map/ppermute | solution.py:24
  108.1 38.9 %collective-permute-start.25 = (f32[128,32]{0,1:T(8,128)S(1)}, f32[128,32]{0,1:T(8,128)S(1)}, u32[]{:S(2)}, u32[]{:S(2)}) collective-permute-start(f32[128,32]{0,1:T(8,128)S(1)} %get-tuple-element.52), channel_id=1, source_target_pairs={{0,2},{1,3},{2,0},{3,1},{4,6},{5,7},{6,4},{7,5},{8,10},{9,11},{10,... | collective-permute-start | bytes 49160 | tf_op jit(solution)/shard_map/ppermute | solution.py:24
  111.9 35.2 %collective-permute-start.26 = (f32[128,32]{0,1:T(8,128)S(1)}, f32[128,32]{0,1:T(8,128)S(1)}, u32[]{:S(2)}, u32[]{:S(2)}) collective-permute-start(f32[128,32]{0,1:T(8,128)S(1)} %get-tuple-element.51), channel_id=1, source_target_pairs={{0,1},{1,2},{2,3},{3,0},{4,5},{5,6},{6,7},{7,4},{8,9},{9,10},{10,1... | collective-permute-start | bytes 49160 | tf_op jit(solution)/shard_map/ppermute | solution.py:24
  124.9 41.4 %collective-permute-start.31 = (bf16[320,1408]{1,0:T(8,128)(2,1)S(1)}, bf16[320,1408]{1,0:T(8,128)(2,1)S(1)}, u32[]{:S(2)}, u32[]{:S(2)}) collective-permute-start(bf16[320,1408]{1,0:T(8,128)(2,1)S(1)} %copy-done.13), channel_id=1, source_target_pairs={{0,2},{1,3},{2,0},{3,1},{4,6},{5,7},{6,4},{7,5},{8,10},{9,11},{10,... | collective-permute-start | bytes 2703368 | tf_op jit(solution)/shard_map/ppermute | solution.py:24
  147.2 16.0 %collective-permute-start.19 = (bf16[96,3,1024]{2,0,1:T(8,128)(2,1)S(1)}, bf16[96,3,1024]{2,0,1:T(8,128)(2,1)S(1)}, u32[]{:S(2)}, u32[]{:S(2)}) collective-permute-start(bf16[96,3,1024]{2,0,1:T(8,128)(2,1)S(1)} %pad_maximum_fusion.2), channel_id=1, source_target_pairs={{0,8},{4,12},{8,0},{12,4},{16,24},{20,28},{24,16},{28,20},{1,9},{5... | collective-permute-start | bytes 1769480 | tf_op jit(solution)/shard_map/ppermute | solution.py:19
  150.9 12.2 %collective-permute-start.28 = (f32[256,32]{0,1:T(8,128)S(1)}, f32[256,32]{0,1:T(8,128)S(1)}, u32[]{:S(2)}, u32[]{:S(2)}) collective-permute-start(f32[256,32]{0,1:T(8,128)S(1)} %pad_maximum_fusion.11), channel_id=1, source_target_pairs={{0,8},{4,12},{8,0},{12,4},{16,24},{20,28},{24,16},{28,20},{1,9},{5... | collective-permute-start | bytes 98312 | tf_op jit(solution)/shard_map/ppermute | solution.py:19
  163.6 6.3 %collective-permute-start.20 = (bf16[192,3,1024]{2,0,1:T(8,128)(2,1)S(1)}, bf16[192,3,1024]{2,0,1:T(8,128)(2,1)S(1)}, u32[]{:S(2)}, u32[]{:S(2)}) collective-permute-start(bf16[192,3,1024]{2,0,1:T(8,128)(2,1)S(1)} %pad_maximum_fusion), channel_id=1, source_target_pairs={{0,4},{4,0},{8,12},{12,8},{16,20},{20,16},{24,28},{28,24},{1,5},{5... | collective-permute-start | bytes 3538952 | tf_op jit(solution)/shard_map/ppermute | solution.py:19
  (24 other events, 307.8 us)

commit v2 on v0

v2 whole, which is shorter than its diff:
```python
import jax
import jax.numpy as jnp
from jax import lax
from jax.experimental import pallas as pl
from jax.sharding import PartitionSpec as P


HIGHEST = lax.Precision.HIGHEST
F32 = jnp.float32
BF16 = jnp.bfloat16
LANES = 128


def dp_groups(size):
    bits = [1 << i for i in range(size.bit_length() - 1)]
    groups = [bits[:1]] + [bits[i : i + 2] for i in range(1, len(bits), 2)]
    return [g for g in groups if g]


def masks_of(group):
    return [sum(b for i, b in enumerate(group) if t >> i & 1) for t in range(1 << len(group))]


def flip(value, mask):
    size = lax.axis_size("dp")
    return lax.ppermute(value, "dp", [(i, i ^ mask) for i in range(size)])


def shift(value, step):
    size = lax.axis_size("expert")
    return lax.ppermute(value, "expert", [(i, (i + step) % size) for i in range(size)])


def place_in(group):
    index = lax.axis_index("dp")
    return sum(((index & bit) != 0).astype(jnp.int32) << i for i, bit in enumerate(group))


def scatter_sum(value):
    for group in dp_groups(lax.axis_size("dp")):
        masks = masks_of(group)
        rows = value.shape[0] // len(masks)
        place = place_in(group)
        block = lambda t: lax.dynamic_slice_in_dim(value, (place ^ t) * rows, rows, 0)
        total = block(0)
        for t in range(1, len(masks)):
            total = total + flip(block(t), masks[t])
        value = total
    return value


def gather_group(value, index, axis):
    group = dp_groups(lax.axis_size("dp"))[index]
    masks = masks_of(group)
    place = place_in(group)
    parts = [value] + [flip(value, masks[t]) for t in range(1, len(masks))]
    return jnp.concatenate([lax.select_n(place ^ t, *parts) if len(parts) > 2 else
                            jnp.where((place ^ t) == 0, parts[0], parts[1])
                            for t in range(len(masks))], axis=axis)


def gather_rows(value, axis=0):
    for i in reversed(range(len(dp_groups(lax.axis_size("dp"))))):
        value = gather_group(value, i, axis)
    return value


def own_block(value, count=None):
    index, size = jnp.int32(0), 1
    for group in dp_groups(lax.axis_size("dp"))[:count]:
        index = index * (1 << len(group)) + place_in(group)
        size <<= len(group)
    rows = value.shape[0] // size
    return lax.dynamic_slice_in_dim(value, index * rows, rows, 0)


def after(value, *others):
    return lax.optimization_barrier((value,) + others)[0]


def split3(value):
    high = value.astype(BF16)
    rest = value - high.astype(F32)
    mid = rest.astype(BF16)
    return high, mid, (rest - mid.astype(F32)).astype(BF16)


def dot3(exact, value, dims):
    out = None
    for term in reversed(split3(value)):
        part = lax.dot_general(exact, term, (dims, ((), ())), preferred_element_type=F32)
        out = part if out is None else out + part
    return out


ROWS_BY_ROWS = ((0,), (0,))
PLAIN = ((1,), (0,))


def rank_kernel(experts, steps, rel_ref, grad_ref, hidden_ref, rank_ref, *out_refs):
    rows = grad_ref.shape[0]
    rel = rel_ref[...]
    group = lax.broadcasted_iota(jnp.int32, (experts, rows), 0)
    onehot = (group == rel).astype(F32)
    before = (
        lax.broadcasted_iota(jnp.int32, (rows, rows), 0) < lax.broadcasted_iota(jnp.int32, (rows, rows), 1)
    ).astype(F32).astype(BF16)
    ranks = jnp.dot(onehot.astype(BF16), before, preferred_element_type=F32)
    rank = jnp.sum(ranks * onehot, axis=0, keepdims=True).astype(jnp.int32)
    rank_ref[...] = rank
    write_packed(rel, rank, steps, grad_ref, hidden_ref, out_refs)


def write_packed(rel, rank, steps, grad_ref, hidden_ref, out_refs):
    rows, width = grad_ref.shape
    for step, out_ref in zip(steps, out_refs):
        capacity = out_ref.shape[0]
        slot = lax.broadcasted_iota(jnp.int32, (capacity, rows), 0)
        target = jnp.where(rel == step, rank, -1)
        pick = (slot == target).astype(F32).astype(BF16)
        out_ref[:, :width] = jnp.dot(pick, grad_ref[...], preferred_element_type=F32).astype(BF16)
        out_ref[:, width:] = jnp.dot(pick, hidden_ref[...], preferred_element_type=F32).astype(BF16)


def pack_kernel(steps, rel_ref, rank_ref, grad_ref, hidden_ref, *out_refs):
    write_packed(rel_ref[...], rank_ref[...], steps, grad_ref, hidden_ref, out_refs)


def left_kernel(rank, grad_ref, hidden_ref, error_ref, q_ref, chosen_ref, out_ref):
    row_q = dot3(grad_ref[...], q_ref[...], PLAIN) * chosen_ref[...]
    own = dot3(error_ref[...], q_ref[:, :rank], PLAIN)
    out_ref[...] = dot3(hidden_ref[...], row_q, ROWS_BY_ROWS)
    out_ref[:, :rank] = out_ref[:, :rank] + own


def orthonormal(left, rank):
    chunk = left.shape[1]
    each = chunk // rank
    full = lax.dot_general(
        left, left, (ROWS_BY_ROWS, ((), ())), precision=HIGHEST, preferred_element_type=F32
    )
    lane = lax.broadcasted_iota(jnp.int32, (rank, chunk), 1)
    row = lax.broadcasted_iota(jnp.int32, (rank, chunk), 0)
    inner = lane % rank
    base = lane - inner
    gram = jnp.zeros((rank, chunk), F32)
    for e in range(each):
        gram = jnp.where(base == e * rank, full[e * rank : (e + 1) * rank, :], gram)
    inverse = (inner == row).astype(F32)
    scale = jnp.zeros((rank, chunk), F32)
    for j in range(rank):
        column = jnp.take_along_axis(gram, base + j, axis=1)
        pivot = 1.0 / column[j : j + 1]
        factor = jnp.where(row > j, column * pivot, 0.0)
        scale = jnp.where(row == j, column[j : j + 1], scale)
        gram, inverse = gram - factor * gram[j : j + 1], inverse - factor * inverse[j : j + 1]
    inverse = inverse * lax.rsqrt(scale)
    wide = jnp.concatenate([inverse] * each, axis=0)
    wide_row = lax.broadcasted_iota(jnp.int32, (chunk, chunk), 0)
    wide_lane = lax.broadcasted_iota(jnp.int32, (chunk, chunk), 1)
    wide = jnp.where(wide_row // rank == wide_lane // rank, wide, 0.0)
    return lax.dot_general(left, wide, (((1,), (1,)), ((), ())), precision=HIGHEST, preferred_element_type=F32)


def right_kernel(rank, left_ref, grad_ref, hidden_ref, error_ref, chosen_ref, own_ref, out_ref):
    lanes = left_ref.shape[1]
    chunk = min(lanes, LANES)
    for start in range(0, lanes, chunk):
        part = slice(start, start + chunk)
        factors = orthonormal(left_ref[:, part], rank)
        row_l = dot3(hidden_ref[...], factors, PLAIN) * chosen_ref[:, part]
        out_ref[:, part] = dot3(grad_ref[...], row_l, ROWS_BY_ROWS)
        if start == 0:
            own_ref[...] = factors[:, :rank]
            own = dot3(error_ref[...], factors[:, :rank], ROWS_BY_ROWS)
            out_ref[:, :rank] = out_ref[:, :rank] + own


def call(kernel, shapes, *args):
    return pl.pallas_call(kernel, out_shape=[jax.ShapeDtypeStruct(s, t) for s, t in shapes])(*args)


def phases(experts):
    steps = list(range(1, experts))
    count = len(steps)
    cuts = [0, (count + 2) // 3, (2 * count + 2) // 3, count]
    return [steps[a:b] for a, b in zip(cuts, cuts[1:])]


def shards(grad_out, hidden_acts, expert_ids, down_weight, error_in, q_prev):
    experts = lax.axis_size("expert")
    replicas = lax.axis_size("dp")
    place = lax.axis_index("expert")
    row_count, width = grad_out.shape
    hidden_width = hidden_acts.shape[1]
    capacity = 2 * row_count // experts
    rank = q_prev.shape[2]
    lanes = experts * rank
    total = width + hidden_width
    rel = lax.rem(place - expert_ids + experts, experts)
    rel_row = rel.reshape(1, row_count)
    weight, q_own, error = down_weight[0], q_prev[0], error_in[0, 0]
    chosen = (lax.broadcasted_iota(jnp.int32, (row_count, lanes), 1) // rank == rel[:, None]).astype(F32)

    steps = list(range(1, experts))
    parts = phases(experts)
    send_rows = lambda packed, ks: [shift(p, -k) for k, p in zip(ks, packed)]
    q_block = own_block(q_own, 1)
    q_blocks = [q_block] + [shift(q_block, k) for k in steps]
    row_rank, *packed = call(
        lambda *refs: rank_kernel(experts, parts[0], *refs),
        [((1, row_count), jnp.int32)] + [((capacity, total), BF16) for _ in parts[0]],
        rel_row, grad_out, hidden_acts,
    )
    recv = send_rows(packed, parts[0])

    q_all = gather_group(jnp.concatenate(q_blocks, axis=1), 0, 0)
    (left_part,) = call(
        lambda *refs: left_kernel(rank, *refs), [((hidden_width, lanes), F32)],
        grad_out, hidden_acts, error, q_all, chosen,
    )
    left_block = scatter_sum(left_part)
    left_sum = left_block
    for k in steps:
        left_sum = left_sum + jnp.roll(shift(left_block, k), k * rank, axis=1)

    weight_block = own_block(weight)
    weight_blocks = jnp.stack([shift(weight_block, k) for k in steps])
    rest = parts[1] + parts[2]
    packed = call(
        lambda *refs: pack_kernel(rest, *refs), [((capacity, total), BF16) for _ in rest],
        rel_row, after(row_rank, left_block), grad_out, hidden_acts,
    )
    recv += send_rows(packed, rest)

    left_sum = gather_rows(left_sum)
    left_own, right_part = call(
        lambda *refs: right_kernel(rank, *refs),
        [((hidden_width, rank), F32), ((width, lanes), F32)],
        left_sum, grad_out, hidden_acts, error, chosen,
    )
    right_block = scatter_sum(right_part)
    right_own = right_block[:, :rank]
    for k in steps:
        right_own = right_own + shift(right_block[:, k * rank : (k + 1) * rank], -k)
    right_factor = gather_rows(right_own) / replicas

    others = gather_rows(weight_blocks, 1)
    rows_back = lambda w: lax.dot_general(grad_out, w, (((1,), (1,)), ((), ())), preferred_element_type=F32)
    grad_hidden = rows_back(weight)
    for k in steps:
        grad_hidden = jnp.where((rel == k)[:, None], rows_back(others[k - 1]), grad_hidden)
    grad_hidden = grad_hidden.astype(BF16)

    own_hidden = jnp.where((rel == 0)[:, None], hidden_acts, jnp.zeros((), BF16))
    rows_product = lambda h, g: lax.dot_general(h, g, (ROWS_BY_ROWS, ((), ())), preferred_element_type=F32)
    merged = error.astype(F32) + rows_product(own_hidden, grad_out)
    for r in recv:
        merged = merged + rows_product(r[:, width:], r[:, :width])
    approx = lax.dot_general(left_own, right_factor, (((1,), (1,)), ((), ())), precision=HIGHEST)
    error_out = (merged - approx).astype(BF16)
    return (grad_hidden, left_own[None], right_factor[None], error_out[None, None])


def solution(mesh):
    placed = (
        P(("dp", "expert"), None),
        P(("dp", "expert"), None),
        P(("dp", "expert")),
        P("expert", None, None),
        P("dp", "expert", None, None),
        P("expert", None, None),
    )
    return jax.shard_map(
        shards,
        mesh=mesh,
        in_specs=placed,
        out_specs=(
            P(("dp", "expert"), None),
            P("expert", None, None),
            P("expert", None, None),
            P("dp", "expert", None, None),
        ),
        check_vma=False,
    )
```

time: 223 us -> 198 us (0.89)
  blocking collectives: 86 us -> 0 us
  starting transfers between devices: 10.1 us -> 47.4 us
  waiting for transfers between devices: 69.4 us -> 94 us
  Pallas kernels: 0 us -> 21.7 us
  between operations: 14.1 us -> 0.98 us
  local copies, waits for them, and re-layouts: 19.1 us -> 9.57 us
    ppermute x0 -> x36, waiting for transfers between devices: none -> 94 us  [the longest x15 75.2 us: shift(): lax.ppermute(value, 'expert', [(i, (i + step) % size) for i in range(size)])]
    all_to_all x1 -> x0, blocking collectives: 62.7 us -> none  [shards(): lax.all_to_all(grad_buffer, 'expert', split_axis=0, concat_axis=0, tiled=...]
    psum x1 -> x0, waiting for transfers between devices: 53.3 us -> none  [shards(): right_factor = lax.psum(right_local, 'dp') / lax.axis_size('dp')]
    ppermute x0 -> x36, starting transfers between devices: none -> 47.4 us  [the longest x15 27.4 us: shift(): lax.ppermute(value, 'expert', [(i, (i + step) % size) for i in range(size)])]
    psum x1 -> x0, blocking collectives: 23.2 us -> none  [shards(): left_sum = lax.psum(left_local, 'dp')]
    pallas_call x0 -> x4, Pallas kernels: none -> 21.7 us  [call(): pl.pallas_call(kernel, out_shape=[jax.ShapeDtypeStruct(s, t) for s, t in...]
    all_to_all x2 -> x0, waiting for transfers between devices: 16.1 us -> none  [the longest x1 16.1 us: shards(): lax.all_to_all(hidden_buffer, 'expert', split_axis=0, concat_axis=0, tile...]
    scatter x2 -> x0, local copies, waits for them, and re-layouts: 15.3 us -> none  [the longest x1 8.24 us: shards(): jnp.zeros((experts * capacity, width), jnp.bfloat16).at[slot_index]]
  transfers between devices with their start and end apart: 3 -> 36, of which waited for: 2 -> 17; matrix products, arithmetic and copies ran while one was open for 9% -> 12% of each run, Pallas kernels for 0% -> 8%
where the time goes in v2:
time: 198 us
  waiting for transfers between devices  94 us (47%)
  starting transfers between devices  47.4 us (24%)
  Pallas kernels  21.7 us (11%)
  matrix products  14.2 us (7%)
  other arithmetic  9.74 us (5%)
  local copies, waits for them, and re-layouts  9.57 us (5%)
    ppermute x15, waiting for transfers between devices, shift(): lax.ppermute(value, 'expert', [(i, (i + step) % size) for i in range(size)])  75.2 us
    ppermute x15, starting transfers between devices, shift(): lax.ppermute(value, 'expert', [(i, (i + step) % size) for i in range(size)])  27.4 us
    pallas_call x4, Pallas kernels, call(): pl.pallas_call(kernel, out_shape=[jax.ShapeDtypeStruct(s, t) for s, t in...  21.7 us
    ppermute x21, starting transfers between devices, flip(): return lax.ppermute(value, 'dp', [(i, i ^ mask) for i in range(size)])  20 us
    ppermute x21, waiting for transfers between devices, flip(): return lax.ppermute(value, 'dp', [(i, i ^ mask) for i in range(size)])  18.7 us
    dot_general x4, matrix products, shards(): lax.dot_general(h, g, (ROWS_BY_ROWS, ((), ())), preferred_element_type=F32)  7.51 us
    dot_general x4, matrix products, shards(): lax.dot_general(grad_out, w, (((1,), (1,)), ((), ())), preferred_element_...  4.08 us
  transfers between devices with their start and end apart: 36, of which 17 were waited for; matrix products, arithmetic and copies ran while one was open for 12% of the time, Pallas kernels for 8%

profile of v2, /device:TPU:0, one launch (start us, length us, event | category | flops | bytes accessed | tf_op | source)
XLA Modules:
  0.0 197.5 jit_solution(18113484311891829442)
XLA Ops:
  1.7 3.1 %collective-permute-start.7 = (f32[512,32]{1,0:T(8,128)S(1)}, f32[512,32]{1,0:T(8,128)S(1)}, u32[]{:S(2)}, u32[]{:S(2)}) collective-permute-start(f32[512,32]{1,0:T(8,128)S(1)} %bitcast.49), channel_id=1, source_target_pairs={{0,1},{1,2},{2,3},{3,0},{4,5},{5,6},{6,7},{7,4},{8,9},{9,10},{10,1... | collective-permute-start | bytes 196616 | tf_op jit(solution)/shard_map/ppermute | solution.py:31
  4.8 2.6 %collective-permute-start.8 = (f32[512,32]{1,0:T(8,128)S(1)}, f32[512,32]{1,0:T(8,128)S(1)}, u32[]{:S(2)}, u32[]{:S(2)}) collective-permute-start(f32[512,32]{1,0:T(8,128)S(1)} %bitcast.50), channel_id=1, source_target_pairs={{0,2},{1,3},{2,0},{3,1},{4,6},{5,7},{6,4},{7,5},{8,10},{9,11},{10,... | collective-permute-start | bytes 196616 | tf_op jit(solution)/shard_map/ppermute | solution.py:31
  9.5 4.7 %collective-permute-done.7 = f32[512,32]{1,0:T(8,128)S(1)} collective-permute-done((f32[512,32]{1,0:T(8,128)S(1)}, f32[512,32]{1,0:T(8,128)S(1)}, u32[]{:S(2)}, u32[]{:S(2)}) %collective-permute-start.7) | collective-permute-done | bytes 65568 | tf_op jit(solution)/shard_map/ppermute | solution.py:31
  14.1 10.4 %collective-permute-done.8 = f32[512,32]{1,0:T(8,128)S(1)} collective-permute-done((f32[512,32]{1,0:T(8,128)S(1)}, f32[512,32]{1,0:T(8,128)S(1)}, u32[]{:S(2)}, u32[]{:S(2)}) %collective-permute-start.8) | collective-permute-done | bytes 65568 | tf_op jit(solution)/shard_map/ppermute | solution.py:31
  27.3 5.7 %shard_map.93 = f32[384,128]{1,0:T(8,128)} custom-call(bf16[640,1024]{1,0:T(8,128)(2,1)} %refs_2_.5, bf16[640,384]{1,0:T(8,128)(2,1)} %refs_3_.1, bf16[384,1024]{1,0:T(8,128)(2,1)} %bitcast.47, f32[1024,128]{1,0:T(8,128)} %pad_maximum_fusion.2.refs_3_, f32[640,128]{1,0:T(8,128)} %fusion.25.refs_4_), custom_call_target="tpu_custom_call" | custom-call | tf_op jit(solution)/shard_map/pallas_call | solution.py:180
  41.5 2.4 %collective-permute-done.14 = f32[48,128]{1,0:T(8,128)S(1)} collective-permute-done((f32[48,128]{1,0:T(8,128)S(1)}, f32[48,128]{1,0:T(8,128)S(1)}, u32[]{:S(2)}, u32[]{:S(2)}) %collective-permute-start.14) | collective-permute-done | bytes 24608 | tf_op jit(solution)/shard_map/ppermute | solution.py:26
  43.9 5.1 %collective-permute-start.16 = (f32[48,128]{1,0:T(8,128)S(1)}, f32[48,128]{1,0:T(8,128)S(1)}, u32[]{:S(2)}, u32[]{:S(2)}) collective-permute-start(f32[48,128]{1,0:T(8,128)S(1)} %add_add_fusion.1), channel_id=1, source_target_pairs={{0,2},{1,3},{2,0},{3,1},{4,6},{5,7},{6,4},{7,5},{8,10},{9,11},{10,... | collective-permute-start | bytes 73736 | tf_op jit(solution)/shard_map/ppermute | solution.py:31
  49.1 2.7 %collective-permute-start = (bf16[48,1024]{1,0:T(8,128)(2,1)S(1)}, bf16[48,1024]{1,0:T(8,128)(2,1)S(1)}, u32[]{:S(2)}, u32[]{:S(2)}) collective-permute-start(bf16[48,1024]{1,0:T(8,128)(2,1)S(1)} %dynamic-slice_bitcast_fusion), channel_id=1, source_target_pairs={{0,1},{1,2},{2,3},{3,0},{4,5},{5,6},{6,7},{7,4},{8,9},{9,10},{10,1... | collective-permute-start | bytes 294920 | tf_op jit(solution)/shard_map/ppermute | solution.py:31
  53.5 3.4 %collective-permute-start.17 = (f32[48,128]{1,0:T(8,128)S(1)}, f32[48,128]{1,0:T(8,128)S(1)}, u32[]{:S(2)}, u32[]{:S(2)}) collective-permute-start(f32[48,128]{1,0:T(8,128)S(1)} %add_add_fusion.1), channel_id=1, source_target_pairs={{0,3},{1,0},{2,1},{3,2},{4,7},{5,4},{6,5},{7,6},{8,11},{9,8},{10,9... | collective-permute-start | bytes 73736 | tf_op jit(solution)/shard_map/ppermute | solution.py:31
  65.3 3.5 %shard_map.95 = (s32[1,640]{1,0:T(1,128)}, bf16[320,1408]{1,0:T(8,128)(2,1)}) custom-call(s32[1,640]{1,0:T(1,128)} %reshape.47.refs_0_, bf16[640,1024]{1,0:T(8,128)(2,1)} %refs_2_.5, bf16[640,384]{1,0:T(8,128)(2,1)} %refs_3_.1), custom_call_target="tpu_custom_call" | custom-call | tf_op jit(solution)/shard_map/pallas_call | solution.py:180
  68.7 3.6 %collective-permute-start.2 = (bf16[48,1024]{1,0:T(8,128)(2,1)S(1)}, bf16[48,1024]{1,0:T(8,128)(2,1)S(1)}, u32[]{:S(2)}, u32[]{:S(2)}) collective-permute-start(bf16[48,1024]{1,0:T(8,128)(2,1)S(1)} %dynamic-slice_bitcast_fusion), channel_id=1, source_target_pairs={{0,3},{1,0},{2,1},{3,2},{4,7},{5,4},{6,5},{7,6},{8,11},{9,8},{10,9... | collective-permute-start | bytes 294920 | tf_op jit(solution)/shard_map/ppermute | solution.py:31
  74.9 8.4 %shard_map.94 = (f32[384,32]{1,0:T(8,128)}, f32[1024,128]{1,0:T(8,128)}) custom-call(f32[384,128]{1,0:T(8,128)} %pad_maximum_fusion.5.refs_0_, bf16[640,1024]{1,0:T(8,128)(2,1)} %refs_2_.5, bf16[640,384]{1,0:T(8,128)(2,1)} %refs_3_.1, bf16[384,1024]{1,0:T(8,128)(2,1)} %bitcast.48, f32[640,128]{1,0:T(8,128)} %fusion.25.refs_4_), custom_call_target="tpu_custom_call" | custom-call | tf_op jit(solution)/shard_map/pallas_call | solution.py:180
  86.1 2.4 %collective-permute-start.5 = (bf16[3,48,1024]{2,1,0:T(8,128)(2,1)S(1)}, bf16[3,48,1024]{2,1,0:T(8,128)(2,1)S(1)}, u32[]{:S(2)}, u32[]{:S(2)}) collective-permute-start(bf16[3,48,1024]{2,1,0:T(8,128)(2,1)S(1)} %pad_maximum_fusion.3), channel_id=1, source_target_pairs={{0,24},{4,28},{8,16},{12,20},{16,8},{20,12},{24,0},{28,4},{1,25},{... | collective-permute-start | bytes 884744 | tf_op jit(solution)/shard_map/ppermute | solution.py:26
  90.1 4.8 %collective-permute-done.3 = bf16[3,48,1024]{2,1,0:T(8,128)(2,1)S(1)} collective-permute-done((bf16[3,48,1024]{2,1,0:T(8,128)(2,1)S(1)}, bf16[3,48,1024]{2,1,0:T(8,128)(2,1)S(1)}, u32[]{:S(2)}, u32[]{:S(2)}) %collective-permute-start.3) | collective-permute-done | bytes 294944 | tf_op jit(solution)/shard_map/ppermute | solution.py:26
  95.4 4.9 %collective-permute-done.4 = bf16[3,48,1024]{2,1,0:T(8,128)(2,1)S(1)} collective-permute-done((bf16[3,48,1024]{2,1,0:T(8,128)(2,1)S(1)}, bf16[3,48,1024]{2,1,0:T(8,128)(2,1)S(1)}, u32[]{:S(2)}, u32[]{:S(2)}) %collective-permute-start.4) | collective-permute-done | bytes 294944 | tf_op jit(solution)/shard_map/ppermute | solution.py:26
  102.7 2.8 %collective-permute-done.25 = f32[128,128]{1,0:T(8,128)S(1)} collective-permute-done((f32[128,128]{1,0:T(8,128)S(1)}, f32[128,128]{1,0:T(8,128)S(1)}, u32[]{:S(2)}, u32[]{:S(2)}) %collective-permute-start.25) | collective-permute-done | bytes 65568 | tf_op jit(solution)/shard_map/ppermute | solution.py:26
  105.8 3.3 %collective-permute-start.27 = (f32[128,32]{1,0:T(8,128)S(1)}, f32[128,32]{1,0:T(8,128)S(1)}, u32[]{:S(2)}, u32[]{:S(2)}) collective-permute-start(f32[128,32]{1,0:T(8,128)S(1)} %get-tuple-element.56), channel_id=1, source_target_pairs={{0,2},{1,3},{2,0},{3,1},{4,6},{5,7},{6,4},{7,5},{8,10},{9,11},{10,... | collective-permute-start | bytes 49160 | tf_op jit(solution)/shard_map/ppermute | solution.py:31
  110.0 2.9 %collective-permute-done.27 = f32[128,32]{1,0:T(8,128)S(1)} collective-permute-done((f32[128,32]{1,0:T(8,128)S(1)}, f32[128,32]{1,0:T(8,128)S(1)}, u32[]{:S(2)}, u32[]{:S(2)}) %collective-permute-start.27) | collective-permute-done | bytes 16416 | tf_op jit(solution)/shard_map/ppermute | solution.py:31
  112.8 2.4 %collective-permute-done.28 = f32[128,32]{1,0:T(8,128)S(1)} collective-permute-done((f32[128,32]{1,0:T(8,128)S(1)}, f32[128,32]{1,0:T(8,128)S(1)}, u32[]{:S(2)}, u32[]{:S(2)}) %collective-permute-start.28) | collective-permute-done | bytes 16416 | tf_op jit(solution)/shard_map/ppermute | solution.py:31
  115.2 3.2 %collective-permute-start.29 = (f32[128,32]{1,0:T(8,128)S(1)}, f32[128,32]{1,0:T(8,128)S(1)}, u32[]{:S(2)}, u32[]{:S(2)}) collective-permute-start(f32[128,32]{1,0:T(8,128)S(1)} %fusion.34), channel_id=1, source_target_pairs={{0,8},{4,12},{8,0},{12,4},{16,24},{20,28},{24,16},{28,20},{1,9},{5... | collective-permute-start | bytes 49160 | tf_op jit(solution)/shard_map/ppermute | solution.py:26
  121.1 4.1 %shard_map.96 = (bf16[320,1408]{1,0:T(8,128)(2,1)}, bf16[320,1408]{1,0:T(8,128)(2,1)}) custom-call(s32[1,640]{1,0:T(1,128)} %reshape.47.refs_0_, s32[1,640]{1,0:T(1,128)} %get-tuple-element.15.refs_1_, bf16[640,1024]{1,0:T(8,128)(2,1)} %refs_2_.5, bf16[640,384]{1,0:T(8,128)(2,1)} %refs_3_.1), custom_call_target="tpu_custom_call" | custom-call | tf_op jit(solution)/shard_map/pallas_call | solution.py:180
  134.0 17.0 %collective-permute-done.35 = bf16[320,1408]{1,0:T(8,128)(2,1)} collective-permute-done((bf16[320,1408]{1,0:T(8,128)(2,1)}, bf16[320,1408]{1,0:T(8,128)(2,1)}, u32[]{:S(2)}, u32[]{:S(2)}) %collective-permute-start.35) | collective-permute-done | bytes 901152 | tf_op jit(solution)/shard_map/ppermute | solution.py:31
  152.8 35.4 %collective-permute-done.34 = bf16[320,1408]{1,0:T(8,128)(2,1)} collective-permute-done((bf16[320,1408]{1,0:T(8,128)(2,1)}, bf16[320,1408]{1,0:T(8,128)(2,1)}, u32[]{:S(2)}, u32[]{:S(2)}) %collective-permute-start.34) | collective-permute-done | bytes 901152 | tf_op jit(solution)/shard_map/ppermute | solution.py:31
  190.0 2.6 %fusion.4 = bf16[1,1,384,1024]{3,2,1,0:T(8,128)(2,1)} fusion(f32[384,1024]{1,0:T(8,128)S(1)} %fusion.16, f32[384,1024]{1,0:T(8,128)S(1)} %fusion.18, f32[384,1024]{1,0:T(8,128)S(1)} %fusion.20, f32[384,1024]{1,0:T(8,128)S(1)} %copy-done.5, f32[384,32]{1,0:T(8,128)S(1)} %copy-done.7, f32[512,32]{0,1:T(8,128)S(1)} %get-tuple-element.46, ...), kind=kOutput, calls=%fused_computation.15 | convolution fusion | flops 153812992 | bytes 8044544 | tf_op jit(solution)/shard_map/dot_general | solution.py:260
  (126 shorter events, 55.2 us)
Async XLA Ops:
  1.7 12.4 %collective-permute-start.7 = (f32[512,32]{1,0:T(8,128)S(1)}, f32[512,32]{1,0:T(8,128)S(1)}, u32[]{:S(2)}, u32[]{:S(2)}) collective-permute-start(f32[512,32]{1,0:T(8,128)S(1)} %bitcast.49), channel_id=1, source_target_pairs={{0,1},{1,2},{2,3},{3,0},{4,5},{5,6},{6,7},{7,4},{8,9},{9,10},{10,1... | collective-permute-start | bytes 196616 | tf_op jit(solution)/shard_map/ppermute | solution.py:31
  4.8 19.7 %collective-permute-start.8 = (f32[512,32]{1,0:T(8,128)S(1)}, f32[512,32]{1,0:T(8,128)S(1)}, u32[]{:S(2)}, u32[]{:S(2)}) collective-permute-start(f32[512,32]{1,0:T(8,128)S(1)} %bitcast.50), channel_id=1, source_target_pairs={{0,2},{1,3},{2,0},{3,1},{4,6},{5,7},{6,4},{7,5},{8,10},{9,11},{10,... | collective-permute-start | bytes 196616 | tf_op jit(solution)/shard_map/ppermute | solution.py:31
  7.4 17.1 %collective-permute-start.9 = (f32[512,32]{1,0:T(8,128)S(1)}, f32[512,32]{1,0:T(8,128)S(1)}, u32[]{:S(2)}, u32[]{:S(2)}) collective-permute-start(f32[512,32]{1,0:T(8,128)S(1)} %bitcast.51), channel_id=1, source_target_pairs={{0,3},{1,0},{2,1},{3,2},{4,7},{5,4},{6,5},{7,6},{8,11},{9,8},{10,9... | collective-permute-start | bytes 196616 | tf_op jit(solution)/shard_map/ppermute | solution.py:31
  43.9 13.0 %collective-permute-start.16 = (f32[48,128]{1,0:T(8,128)S(1)}, f32[48,128]{1,0:T(8,128)S(1)}, u32[]{:S(2)}, u32[]{:S(2)}) collective-permute-start(f32[48,128]{1,0:T(8,128)S(1)} %add_add_fusion.1), channel_id=1, source_target_pairs={{0,2},{1,3},{2,0},{3,1},{4,6},{5,7},{6,4},{7,5},{8,10},{9,11},{10,... | collective-permute-start | bytes 73736 | tf_op jit(solution)/shard_map/ppermute | solution.py:31
  49.1 35.8 %collective-permute-start = (bf16[48,1024]{1,0:T(8,128)(2,1)S(1)}, bf16[48,1024]{1,0:T(8,128)(2,1)S(1)}, u32[]{:S(2)}, u32[]{:S(2)}) collective-permute-start(bf16[48,1024]{1,0:T(8,128)(2,1)S(1)} %dynamic-slice_bitcast_fusion), channel_id=1, source_target_pairs={{0,1},{1,2},{2,3},{3,0},{4,5},{5,6},{6,7},{7,4},{8,9},{9,10},{10,1... | collective-permute-start | bytes 294920 | tf_op jit(solution)/shard_map/ppermute | solution.py:31
  51.7 33.2 %collective-permute-start.1 = (bf16[48,1024]{1,0:T(8,128)(2,1)S(1)}, bf16[48,1024]{1,0:T(8,128)(2,1)S(1)}, u32[]{:S(2)}, u32[]{:S(2)}) collective-permute-start(bf16[48,1024]{1,0:T(8,128)(2,1)S(1)} %dynamic-slice_bitcast_fusion), channel_id=1, source_target_pairs={{0,2},{1,3},{2,0},{3,1},{4,6},{5,7},{6,4},{7,5},{8,10},{9,11},{10,... | collective-permute-start | bytes 294920 | tf_op jit(solution)/shard_map/ppermute | solution.py:31
  59.0 9.7 %collective-permute-start.18 = (f32[48,128]{1,0:T(8,128)S(1)}, f32[48,128]{1,0:T(8,128)S(1)}, u32[]{:S(2)}, u32[]{:S(2)}) collective-permute-start(f32[48,128]{1,0:T(8,128)S(1)} %fusion.37), channel_id=1, source_target_pairs={{0,8},{4,12},{8,0},{12,4},{16,24},{20,28},{24,16},{28,20},{1,9},{5... | collective-permute-start | bytes 73736 | tf_op jit(solution)/shard_map/ppermute | solution.py:26
  59.6 12.8 %collective-permute-start.19 = (f32[48,128]{1,0:T(8,128)S(1)}, f32[48,128]{1,0:T(8,128)S(1)}, u32[]{:S(2)}, u32[]{:S(2)}) collective-permute-start(f32[48,128]{1,0:T(8,128)S(1)} %fusion.37), channel_id=1, source_target_pairs={{0,16},{4,20},{8,24},{12,28},{16,0},{20,4},{24,8},{28,12},{1,17},{... | collective-permute-start | bytes 73736 | tf_op jit(solution)/shard_map/ppermute | solution.py:26
  60.3 12.2 %collective-permute-start.20 = (f32[48,128]{1,0:T(8,128)S(1)}, f32[48,128]{1,0:T(8,128)S(1)}, u32[]{:S(2)}, u32[]{:S(2)}) collective-permute-start(f32[48,128]{1,0:T(8,128)S(1)} %fusion.37), channel_id=1, source_target_pairs={{0,24},{4,28},{8,16},{12,20},{16,8},{20,12},{24,0},{28,4},{1,25},{... | collective-permute-start | bytes 73736 | tf_op jit(solution)/shard_map/ppermute | solution.py:26
  68.7 16.2 %collective-permute-start.2 = (bf16[48,1024]{1,0:T(8,128)(2,1)S(1)}, bf16[48,1024]{1,0:T(8,128)(2,1)S(1)}, u32[]{:S(2)}, u32[]{:S(2)}) collective-permute-start(bf16[48,1024]{1,0:T(8,128)(2,1)S(1)} %dynamic-slice_bitcast_fusion), channel_id=1, source_target_pairs={{0,3},{1,0},{2,1},{3,2},{4,7},{5,4},{6,5},{7,6},{8,11},{9,8},{10,9... | collective-permute-start | bytes 294920 | tf_op jit(solution)/shard_map/ppermute | solution.py:31
  72.4 59.1 %collective-permute-start.33 = (bf16[320,1408]{1,0:T(8,128)(2,1)}, bf16[320,1408]{1,0:T(8,128)(2,1)}, u32[]{:S(2)}, u32[]{:S(2)}) collective-permute-start(bf16[320,1408]{1,0:T(8,128)(2,1)} %get-tuple-element.13), channel_id=1, source_target_pairs={{0,3},{1,0},{2,1},{3,2},{4,7},{5,4},{6,5},{7,6},{8,11},{9,8},{10,9... | collective-permute-start | bytes 2703368 | tf_op jit(solution)/shard_map/ppermute | solution.py:31
  85.0 9.9 %collective-permute-start.3 = (bf16[3,48,1024]{2,1,0:T(8,128)(2,1)S(1)}, bf16[3,48,1024]{2,1,0:T(8,128)(2,1)S(1)}, u32[]{:S(2)}, u32[]{:S(2)}) collective-permute-start(bf16[3,48,1024]{2,1,0:T(8,128)(2,1)S(1)} %pad_maximum_fusion.3), channel_id=1, source_target_pairs={{0,8},{4,12},{8,0},{12,4},{16,24},{20,28},{24,16},{28,20},{1,9},{5... | collective-permute-start | bytes 884744 | tf_op jit(solution)/shard_map/ppermute | solution.py:26
  85.6 14.8 %collective-permute-start.4 = (bf16[3,48,1024]{2,1,0:T(8,128)(2,1)S(1)}, bf16[3,48,1024]{2,1,0:T(8,128)(2,1)S(1)}, u32[]{:S(2)}, u32[]{:S(2)}) collective-permute-start(bf16[3,48,1024]{2,1,0:T(8,128)(2,1)S(1)} %pad_maximum_fusion.3), channel_id=1, source_target_pairs={{0,16},{4,20},{8,24},{12,28},{16,0},{20,4},{24,8},{28,12},{1,17},{... | collective-permute-start | bytes 884744 | tf_op jit(solution)/shard_map/ppermute | solution.py:26
  86.1 16.4 %collective-permute-start.5 = (bf16[3,48,1024]{2,1,0:T(8,128)(2,1)S(1)}, bf16[3,48,1024]{2,1,0:T(8,128)(2,1)S(1)}, u32[]{:S(2)}, u32[]{:S(2)}) collective-permute-start(bf16[3,48,1024]{2,1,0:T(8,128)(2,1)S(1)} %pad_maximum_fusion.3), channel_id=1, source_target_pairs={{0,24},{4,28},{8,16},{12,20},{16,8},{20,12},{24,0},{28,4},{1,25},{... | collective-permute-start | bytes 884744 | tf_op jit(solution)/shard_map/ppermute | solution.py:26
  89.5 13.0 %collective-permute-start.23 = (f32[128,128]{1,0:T(8,128)S(1)}, f32[128,128]{1,0:T(8,128)S(1)}, u32[]{:S(2)}, u32[]{:S(2)}) collective-permute-start(f32[128,128]{1,0:T(8,128)S(1)} %get-tuple-element.40), channel_id=1, source_target_pairs={{0,8},{4,12},{8,0},{12,4},{16,24},{20,28},{24,16},{28,20},{1,9},{5... | collective-permute-start | bytes 196616 | tf_op jit(solution)/shard_map/ppermute | solution.py:26
  94.9 7.8 %collective-permute-start.24 = (f32[128,128]{1,0:T(8,128)S(1)}, f32[128,128]{1,0:T(8,128)S(1)}, u32[]{:S(2)}, u32[]{:S(2)}) collective-permute-start(f32[128,128]{1,0:T(8,128)S(1)} %get-tuple-element.42), channel_id=1, source_target_pairs={{0,16},{4,20},{8,24},{12,28},{16,0},{20,4},{24,8},{28,12},{1,17},{... | collective-permute-start | bytes 196616 | tf_op jit(solution)/shard_map/ppermute | solution.py:26
  105.8 7.0 %collective-permute-start.27 = (f32[128,32]{1,0:T(8,128)S(1)}, f32[128,32]{1,0:T(8,128)S(1)}, u32[]{:S(2)}, u32[]{:S(2)}) collective-permute-start(f32[128,32]{1,0:T(8,128)S(1)} %get-tuple-element.56), channel_id=1, source_target_pairs={{0,2},{1,3},{2,0},{3,1},{4,6},{5,7},{6,4},{7,5},{8,10},{9,11},{10,... | collective-permute-start | bytes 49160 | tf_op jit(solution)/shard_map/ppermute | solution.py:31
  109.1 6.1 %collective-permute-start.28 = (f32[128,32]{1,0:T(8,128)S(1)}, f32[128,32]{1,0:T(8,128)S(1)}, u32[]{:S(2)}, u32[]{:S(2)}) collective-permute-start(f32[128,32]{1,0:T(8,128)S(1)} %get-tuple-element.55), channel_id=1, source_target_pairs={{0,1},{1,2},{2,3},{3,0},{4,5},{5,6},{6,7},{7,4},{8,9},{9,10},{10,1... | collective-permute-start | bytes 49160 | tf_op jit(solution)/shard_map/ppermute | solution.py:31
  115.2 10.6 %collective-permute-start.29 = (f32[128,32]{1,0:T(8,128)S(1)}, f32[128,32]{1,0:T(8,128)S(1)}, u32[]{:S(2)}, u32[]{:S(2)}) collective-permute-start(f32[128,32]{1,0:T(8,128)S(1)} %fusion.34), channel_id=1, source_target_pairs={{0,8},{4,12},{8,0},{12,4},{16,24},{20,28},{24,16},{28,20},{1,9},{5... | collective-permute-start | bytes 49160 | tf_op jit(solution)/shard_map/ppermute | solution.py:26
  118.4 7.5 %collective-permute-start.30 = (f32[128,32]{1,0:T(8,128)S(1)}, f32[128,32]{1,0:T(8,128)}, u32[]{:S(2)}, u32[]{:S(2)}) collective-permute-start(f32[128,32]{1,0:T(8,128)S(1)} %fusion.34), channel_id=1, source_target_pairs={{0,16},{4,20},{8,24},{12,28},{16,0},{20,4},{24,8},{28,12},{1,17},{... | collective-permute-start | bytes 49160 | tf_op jit(solution)/shard_map/ppermute | solution.py:26
  118.4 8.1 %collective-permute-start.31 = (f32[128,32]{1,0:T(8,128)S(1)}, f32[128,32]{1,0:T(8,128)}, u32[]{:S(2)}, u32[]{:S(2)}) collective-permute-start(f32[128,32]{1,0:T(8,128)S(1)} %fusion.34), channel_id=1, source_target_pairs={{0,24},{4,28},{8,16},{12,20},{16,8},{20,12},{24,0},{28,4},{1,25},{... | collective-permute-start | bytes 49160 | tf_op jit(solution)/shard_map/ppermute | solution.py:26
  121.0 71.6 %collective-permute-start.6 = (bf16[3,192,1024]{2,1,0:T(8,128)(2,1)}, bf16[3,192,1024]{2,1,0:T(8,128)(2,1)S(1)}, u32[]{:S(2)}, u32[]{:S(2)}) collective-permute-start(bf16[3,192,1024]{2,1,0:T(8,128)(2,1)} %pad_maximum_fusion), channel_id=1, source_target_pairs={{0,4},{4,0},{8,12},{12,8},{16,20},{20,16},{24,28},{28,24},{1,5},{5... | collective-permute-start | bytes 3538952 | tf_op jit(solution)/shard_map/ppermute | solution.py:26
  125.9 25.1 %collective-permute-start.35 = (bf16[320,1408]{1,0:T(8,128)(2,1)}, bf16[320,1408]{1,0:T(8,128)(2,1)}, u32[]{:S(2)}, u32[]{:S(2)}) collective-permute-start(bf16[320,1408]{1,0:T(8,128)(2,1)} %get-tuple-element.17), channel_id=1, source_target_pairs={{0,1},{1,2},{2,3},{3,0},{4,5},{5,6},{6,7},{7,4},{8,9},{9,10},{10,1... | collective-permute-start | bytes 2703368 | tf_op jit(solution)/shard_map/ppermute | solution.py:31
  125.9 62.3 %collective-permute-start.34 = (bf16[320,1408]{1,0:T(8,128)(2,1)}, bf16[320,1408]{1,0:T(8,128)(2,1)}, u32[]{:S(2)}, u32[]{:S(2)}) collective-permute-start(bf16[320,1408]{1,0:T(8,128)(2,1)} %get-tuple-element.16), channel_id=1, source_target_pairs={{0,2},{1,3},{2,0},{3,1},{4,6},{5,7},{6,4},{7,5},{8,10},{9,11},{10,... | collective-permute-start | bytes 2703368 | tf_op jit(solution)/shard_map/ppermute | solution.py:31
  (22 other events, 254.2 us)
